TPU v7x, 32 devices: a whole 2x2x4 slice. The times are simulated.
32 devices in a mesh: wide: 8 (over z, core), narrow: 4 (over y, x).
Axes of the slice: x: 2, y: 2, z: 4, core: 2. Of those that a mesh axis runs over, the one named last changes fastest.
Arguments:
- activations: bfloat16 [512, 16384], P(None, 'wide'), may hold values from -6 to 6
- enc_weight: bfloat16 [16384, 4096], P('wide', 'narrow'), may hold values from -0.046875 to 0.046875
- enc_bias: float32 [4096], P('narrow'), may hold values from -4 to 4
- dec_weight: bfloat16 [4096, 16384], P('narrow', 'wide'), may hold values from -0.375 to 0.375
- dec_bias: float32 [16384], P('wide'), may hold values from -4 to 4
- active_ids: int32 [512, 64], replicated, may hold values from 0 to 4095, all different within a row
Outputs:
- dec_grad: bfloat16 [4096, 16384], P('narrow', 'wide')
- latent_grad: float32 [512, 4096], P('wide', 'narrow')
Inputs may be any that keep to these rules, and one draw needn't show every extreme that they name: `active_ids`: each row names 64 different latents; every latent is named by some row.
All inputs are finite; a program needn't handle non-finite values.
Results may differ from a plain program's by a relative error of at most 0.0058.
Values may be sent and summed in bfloat16 or wider, within the bound.
A program may use at most 128 MiB of HBM per device.

v0:
```python
import jax
import jax.numpy as jnp
from jax import lax
from jax.sharding import PartitionSpec as P


def prefix(value, axis, combine, identity):
    length, position = (lax.axis_size(axis), lax.axis_index(axis))
    everything = jax.tree.map(
        lambda part, kind: lax.all_gather(part.astype(kind), axis),
        value,
        (jnp.bfloat16, jnp.bfloat16),
    )
    start = jax.tree.map(
        lambda part, zero: jnp.broadcast_to(jnp.asarray(zero, part.dtype), part.shape),
        value,
        identity,
    )

    def hop(k, before):
        reached = k < position
        new = combine(
            before, jax.tree.map(lambda part, own: part[k].astype(own.dtype), everything, value)
        )
        return jax.tree.map(lambda a, b: jnp.where(reached, a, b), new, before)

    return lax.fori_loop(0, length, hop, start)


def add_fields(earlier, later):
    return jax.tree.map(jnp.add, earlier, later)


def local(activations, enc_weight, enc_bias, dec_weight, dec_bias, active_ids):
    token_count = activations.shape[0]
    latent_width = enc_weight.shape[1]
    groups = lax.axis_size("narrow")
    group_index = lax.axis_index("narrow")
    first_latent = group_index * latent_width
    inside = (active_ids >= first_latent) & (active_ids < first_latent + latent_width)
    local_ids = jnp.where(inside, active_ids - first_latent, latent_width)
    row_index = jnp.arange(token_count, dtype=jnp.int32)[:, None]
    active_mask = (
        jnp.zeros((token_count, latent_width), jnp.float32)
        .at[row_index, local_ids]
        .set(1.0, mode="drop")
    )
    share_rows = token_count // lax.axis_size("wide")
    offset = lax.axis_index("wide") * share_rows
    own_mask = lax.dynamic_slice_in_dim(active_mask, offset, share_rows, 0)
    partial_pre = jnp.dot(activations, enc_weight, preferred_element_type=jnp.float32)
    preact = lax.psum(partial_pre, "wide") + enc_bias
    latents = (active_mask * preact).astype(jnp.bfloat16)
    recon_part = jnp.dot(latents, dec_weight, preferred_element_type=jnp.float32)
    target = activations.astype(jnp.float32)
    nothing = jnp.zeros_like(recon_part)
    position = group_index.astype(jnp.float32)
    lower_sum, lower_weighted = prefix(
        (recon_part, position * recon_part), "narrow", add_fields, (nothing, nothing)
    )
    weighted_sum = lax.psum((groups - position) * recon_part, "narrow")
    suffix = (
        (groups - position) * dec_bias
        + weighted_sum
        - position * lower_sum
        + lower_weighted
        - (groups - position) * target
    )
    errors = (suffix / groups).astype(jnp.bfloat16)
    dec_grad = lax.dot_general(
        latents, errors, (((0,), (0,)), ((), ())), preferred_element_type=jnp.float32
    ).astype(jnp.bfloat16)
    latent_rows = lax.psum_scatter(
        lax.dot_general(
            errors, dec_weight, (((1,), (1,)), ((), ())), preferred_element_type=jnp.float32
        ),
        "wide",
        scatter_dimension=0,
        tiled=True,
    )
    latent_out = own_mask * latent_rows
    return (dec_grad, latent_out)


def solution(mesh):
    in_specs = (
        P(None, "wide"),
        P("wide", "narrow"),
        P("narrow"),
        P("narrow", "wide"),
        P("wide"),
        P(),
    )
    out_specs = (P("narrow", "wide"), P("wide", "narrow"))
    return jax.shard_map(local, mesh=mesh, in_specs=in_specs, out_specs=out_specs, check_vma=False)
```

profile of v0, /device:TPU:0, one launch (start us, length us, event | category | flops | bytes accessed | tf_op | source)
XLA Modules:
  0.0 489.2 jit_solution(10238089520648462262)
XLA Ops:
  7.2 0.0 copy-start.5
  7.2 0.0 copy-start.4
  7.2 0.0 copy-start.1
  7.2 0.0 all-reduce.3.cloned.1.call-start
  7.2 6.5 %fusion.3 = f32[512,1024]{1,0:T(8,128)} fusion(bf16[512,2048]{1,0:T(8,128)(2,1)} %param.8, bf16[2048,1024]{1,0:T(8,128)(2,1)} %param.9), kind=kOutput, calls=%fused_computation.18 | convolution fusion | flops 2147483648 | bytes 8388608 | tf_op jit(solution)/shard_map/dot_general | solution.py:51
  13.7 0.0 all-reduce.3.cloned.1.call-update
  13.8 0.0 all-gather.5.cloned.1.call-start
  13.8 0.0 copy-done.1
  13.9 0.0 copy-start.3
  13.9 0.0 copy-done.5
  13.9 0.1 multiply_reduce_fusion
  14.0 0.0 copy-done.4
  14.0 0.1 and_reduce_fusion
  14.2 0.1 copy.8
  14.3 0.1 reshape.18
  14.4 121.4 %scatter_custom_fusion = f32[524288]{0:T(1024)} fusion(s32[32768]{0:T(1024)S(1)} %reshape.18, f32[32768]{0:T(1024)S(1)} %broadcast.15, f32[]{:T(128)} %constant.43.clone.1), kind=kCustom, calls=%fused_computation.8 | custom fusion | bytes 2097156
  135.9 1.7 reshape.15
  137.6 0.0 all-reduce.3.cloned.1.call-done
  137.6 0.0 copy-done.3
  137.6 0.0 copy-start.6
  137.7 2.2 multiply_convert_fusion.2
  139.9 0.6 copy-done.6
  140.5 5.6 %broadcast_multiply_fusion = (f32[512,2048]{1,0:T(8,128)}, bf16[512,2048]{1,0:T(8,128)(2,1)}, bf16[512,2048]{1,0:T(8,128)(2,1)}) fusion(f32[]{:T(128)S(6)} %sub.16, f32[]{:T(128)S(6)} %convert_element_type.42, bf16[512,1024]{1,0:T(8,128)(2,1)S(1)} %multiply_convert_fusion.2, bf16[1024,2048]{1,0:T(8,128)(2,1)S(1)} %copy-done.6), kind=kOutput, calls=%fused_computation.6 | convolution fusion | flops 2151677952 | bytes 13631496 | tf_op jit(solution)/shard_map/dot_general | solution.py:54
  146.1 0.0 copy-start.2
  146.1 0.0 all-gather.5.cloned.1.call-update
  146.1 0.0 all-gather.7.cloned.1.call-start
  146.2 0.7 all-gather.7.cloned.1.call-update
  146.9 0.0 all-reduce.5.cloned.1.call-start
  146.9 0.5 all-reduce.5.cloned.1.call-update
  147.4 0.2 reduce-scatter.2.cloned.1.call-start
  147.7 0.0 copy-done.2
  147.7 88.8 %all-gather.5.cloned.1.call-done = bf16[2048,2048]{1,0:T(8,128)(2,1)} async-done(((bf16[512,2048]{1,0:T(8,128)(2,1)}), bf16[2048,2048]{1,0:T(8,128)(2,1)}) %all-gather.5.cloned.1.call-update) | async-done | bytes 8388624 | tf_op jit(solution)/shard_map/all_gather | solution.py:10
  236.5 89.4 %all-gather.7.cloned.1.call-done = bf16[2048,2048]{1,0:T(8,128)(2,1)} async-done(((bf16[512,2048]{1,0:T(8,128)(2,1)}), bf16[2048,2048]{1,0:T(8,128)(2,1)}) %all-gather.7.cloned.1.call-update) | async-done | bytes 8388624 | tf_op jit(solution)/shard_map/all_gather | solution.py:10
  325.8 39.3 %while.16 = (s32[]{:T(128)}, f32[512,2048]{1,0:T(8,128)}, f32[512,2048]{1,0:T(8,128)}, s32[]{:T(128)}, bf16[4,512,2048]{2,1,0:T(8,128)(2,1)}, /*index=5*/bf16[4,512,2048]{2,1,0:T(8,128)(2,1)}, s32[]{:T(128)}, s32[]{:T(128)}) while((s32[]{:T(128)}, f32[512,2048]{1,0:T(8,128)}, f32[512,2048]{1,0:T(8,128)}, s32[]{:T(128)}, ...), condition=%wide.region_4.5_spmd.clone, body=%wide.region_3.4_spmd.clone.sunk | while | flops 8388612 | bytes 20971628 | solution.py:27
  325.8 7.8 %add_select_fusion.3 = (f32[512,2048]{1,0:T(8,128)}, f32[512,2048]{1,0:T(8,128)}) fusion(f32[512,2048]{1,0:T(8,128)} %get-tuple-element.204, bf16[4,512,2048]{2,1,0:T(8,128)(2,1)} %get-tuple-element.215, s32[]{:T(128)} %get-tuple-element.202, pred[]{:T(512)S(6)} %compare.7, pred[]{:T(512)S(6)} %lt.50, bf16[4,512,2048]{2,1,0:T(8,128)(2,1)} %get-tuple-element.214, ...), kind=kLoop, calls=%fused_computation.1.clone.1 | loop fusion | flops 8388608 | bytes 20971526 | tf_op jit(solution)/shard_map/while/body/eval_jaxpr/jit(_where)/select_n | solution.py:25
  333.6 10.8 %add_select_fusion.3 = (f32[512,2048]{1,0:T(8,128)}, f32[512,2048]{1,0:T(8,128)}) fusion(f32[512,2048]{1,0:T(8,128)} %get-tuple-element.204, bf16[4,512,2048]{2,1,0:T(8,128)(2,1)} %get-tuple-element.215, s32[]{:T(128)} %get-tuple-element.202, pred[]{:T(512)S(6)} %compare.7, pred[]{:T(512)S(6)} %lt.50, bf16[4,512,2048]{2,1,0:T(8,128)(2,1)} %get-tuple-element.214, ...), kind=kLoop, calls=%fused_computation.1.clone.1 | loop fusion | flops 8388608 | bytes 20971526 | tf_op jit(solution)/shard_map/while/body/eval_jaxpr/jit(_where)/select_n | solution.py:25
  344.4 10.4 %add_select_fusion.3 = (f32[512,2048]{1,0:T(8,128)}, f32[512,2048]{1,0:T(8,128)}) fusion(f32[512,2048]{1,0:T(8,128)} %get-tuple-element.204, bf16[4,512,2048]{2,1,0:T(8,128)(2,1)} %get-tuple-element.215, s32[]{:T(128)} %get-tuple-element.202, pred[]{:T(512)S(6)} %compare.7, pred[]{:T(512)S(6)} %lt.50, bf16[4,512,2048]{2,1,0:T(8,128)(2,1)} %get-tuple-element.214, ...), kind=kLoop, calls=%fused_computation.1.clone.1 | loop fusion | flops 8388608 | bytes 20971526 | tf_op jit(solution)/shard_map/while/body/eval_jaxpr/jit(_where)/select_n | solution.py:25
  354.8 10.3 %add_select_fusion.3 = (f32[512,2048]{1,0:T(8,128)}, f32[512,2048]{1,0:T(8,128)}) fusion(f32[512,2048]{1,0:T(8,128)} %get-tuple-element.204, bf16[4,512,2048]{2,1,0:T(8,128)(2,1)} %get-tuple-element.215, s32[]{:T(128)} %get-tuple-element.202, pred[]{:T(512)S(6)} %compare.7, pred[]{:T(512)S(6)} %lt.50, bf16[4,512,2048]{2,1,0:T(8,128)(2,1)} %get-tuple-element.214, ...), kind=kLoop, calls=%fused_computation.1.clone.1 | loop fusion | flops 8388608 | bytes 20971526 | tf_op jit(solution)/shard_map/while/body/eval_jaxpr/jit(_where)/select_n | solution.py:25
  365.1 67.5 %all-reduce.5.cloned.1.call-done = f32[512,2048]{1,0:T(8,128)} async-done(((f32[512,2048]{1,0:T(8,128)}), f32[512,2048]{1,0:T(8,128)}) %all-reduce.5.cloned.1.call-update) | async-done | bytes 4194320 | tf_op jit(solution)/shard_map/psum | solution.py:61
  432.6 0.0 copy-start.7
  432.6 7.2 %multiply_convert_fusion = bf16[512,2048]{1,0:T(8,128)(2,1)S(1)} fusion(bf16[512,2048]{1,0:T(8,128)(2,1)} %param.8, f32[512,2048]{1,0:T(8,128)} %get-tuple-element.113, f32[512,2048]{1,0:T(8,128)} %get-tuple-element.112, f32[512,2048]{1,0:T(8,128)} %all-reduce.5.cloned.1.call-done, f32[]{:T(128)S(6)} %convert_element_type.42, f32[]{:T(128)S(6)} %sub.16, ...), kind=kLoop, calls=%fused_computation.3 | loop fusion | flops 9437184 | bytes 16785416 | tf_op jit(solution)/shard_map/convert_element_type | solution.py:69
  439.8 0.0 copy-start
  439.8 1.3 copy-done
  441.1 0.0 copy-done.7
  441.1 3.7 fusion.4
  444.8 0.0 reduce-scatter.2.cloned.1.call-update
  444.8 6.0 %convolution_convert_fusion = bf16[1024,2048]{1,0:T(8,128)(2,1)} fusion(bf16[512,1024]{1,0:T(8,128)(2,1)S(1)} %multiply_convert_fusion.2, bf16[512,2048]{1,0:T(8,128)(2,1)} %copy-done), kind=kOutput, calls=%fused_computation.5 | convolution fusion | flops 2149580800 | bytes 7340032 | tf_op jit(solution)/shard_map/dot_general | solution.py:70
  450.8 30.2 %reduce-scatter.2.cloned.1.call-done = f32[64,1024]{1,0:T(8,128)} async-done(((f32[512,1024]{1,0:T(8,128)}), f32[64,1024]{1,0:T(8,128)}) %reduce-scatter.2.cloned.1.call-update) | async-done | bytes 262160 | tf_op jit(solution)/shard_map/reduce_scatter | solution.py:73
  481.0 1.7 dynamic-slice_multiply_fusion
  (7 shorter events, 0.1 us)
Async XLA Ops:
  7.2 6.8 %copy-start.5 = (s32[2]{0:T(128)S(1)}, s32[2]{0:T(128)}, u32[]{:S(2)}) copy-start(s32[2]{0:T(128)} %constant.54) | copy-start | bytes 28
  7.2 6.8 %copy-start.4 = (s32[2]{0:T(128)S(1)}, s32[2]{0:T(128)}, u32[]{:S(2)}) copy-start(s32[2]{0:T(128)} %constant.57) | copy-start | bytes 28
  7.2 6.6 %copy-start.1 = (s32[512,64]{0,1:T(8,128)S(1)}, s32[512,64]{0,1:T(8,128)}, u32[]{:S(2)}) copy-start(s32[512,64]{0,1:T(8,128)} %param.13) | copy-start | bytes 393220
  7.2 130.4 %all-reduce.3.cloned.1.call-start = ((), (), s32[]{:S(2)}) async-start(), calls=%async_computation.1 | async-start | bytes 4194304 | tf_op jit(solution)/shard_map/psum | solution.py:52
  13.8 222.7 %all-gather.5.cloned.1.call-start = ((), (), s32[]{:S(2)}) async-start(), calls=%async_computation.4 | async-start | bytes 10485760 | tf_op jit(solution)/shard_map/all_gather | solution.py:10
  13.9 123.8 %copy-start.3 = (f32[1024]{0:T(1024)S(1)}, f32[1024]{0:T(1024)}, u32[]{:S(2)}) copy-start(f32[1024]{0:T(1024)} %param.10) | copy-start | bytes 12292
  137.6 2.8 copy-start.6
  146.1 1.6 copy-start.2
  146.1 179.7 %all-gather.7.cloned.1.call-start = ((), (), s32[]{:S(2)}) async-start(), calls=%async_computation.5 | async-start | bytes 10485760 | tf_op jit(solution)/shard_map/all_gather | solution.py:10
  146.9 285.8 %all-reduce.5.cloned.1.call-start = ((), (), s32[]{:S(2)}) async-start(), calls=%async_computation.2 | async-start | bytes 8388608 | tf_op jit(solution)/shard_map/psum | solution.py:61
  147.4 333.6 %reduce-scatter.2.cloned.1.call-start = ((), (), s32[]{:S(2)}) async-start(), calls=%async_computation.3 | async-start | bytes 2359296 | tf_op jit(solution)/shard_map/reduce_scatter | solution.py:73
  432.6 8.5 %copy-start.7 = (bf16[1024,2048]{1,0:T(8,128)(2,1)S(1)}, bf16[1024,2048]{1,0:T(8,128)(2,1)}, u32[]{:S(2)}) copy-start(bf16[1024,2048]{1,0:T(8,128)(2,1)} %param.11) | copy-start | bytes 12582916
  439.8 1.3 copy-start
Sparse Core Ops, SparseCore 0:
  13.9 67.9 all-reduce.2
  146.2 90.1 all-gather.4
  238.3 87.4 all-gather.6
  329.0 103.5 all-reduce.4
  445.0 35.9 reduce-scatter.1
where the time goes:
time: 489 us
  waiting for transfers between devices  277 us (57%)
  local copies, waits for them, and re-layouts  125 us (26%)
  other arithmetic  50.6 us (10%)
  matrix products  21.8 us (4%)
  between operations  14 us (3%)
    all_gather x2, waiting for transfers between devices, prefix(): lax.all_gather(part.astype(kind), axis)  178 us
    unnamed x20, local copies, waits for them, and re-layouts  124 us
    psum x1, waiting for transfers between devices, local(): weighted_sum = lax.psum((groups - position) * recon_part, 'narrow')  67.5 us
    select_n x4, other arithmetic, hop(): return jax.tree.map(lambda a, b: jnp.where(reached, a, b), new, before)  39.3 us
    reduce_scatter x1, waiting for transfers between devices, local(): lax.psum_scatter(lax.dot_general(errors, dec_weight, (((1,), (1,)), ((),...  30.2 us
  transfers between devices with their start and end apart: 5, of which 4 were waited for; matrix products, arithmetic and copies ran while one was open for 35% of the time, Pallas kernels for 0%

commit v1 on v0

v1 whole, which is shorter than its diff:
```python
import functools

import jax
import jax.numpy as jnp
from jax import lax
from jax.experimental import pallas as pl
from jax.experimental.pallas import tpu as pltpu
from jax.sharding import PartitionSpec as P

LANES = 128
SUBLANES = 8
MESH = pl.DeviceIdType.MESH


def lookup(table, index):
    return jnp.take_along_axis(table, index, axis=1, mode="promise_in_bounds")


def pick_active(dense_ref, ids, first_row, rows, fold, top):
    tile, lane = ids >> 7, ids & (LANES - 1)
    half = lax.broadcasted_iota(jnp.int32, ids.shape, 1) // top
    picked = jnp.zeros(ids.shape, jnp.float32)
    for part in range(fold):
        here = jnp.where(half == part, tile, -1)
        for j in range(dense_ref.shape[1] // LANES):
            start = first_row + part * rows
            table = dense_ref[pl.ds(start, rows), j * LANES : (j + 1) * LANES]
            picked = jnp.where(here == j, lookup(table, lane), picked)
    return picked


def encode_kernel(steps, fold, top, act_ref, enc_ref, bias_ref, ids_ref, out_ref, total):
    step = pl.program_id(0)
    product = jnp.dot(act_ref[...], enc_ref[...], preferred_element_type=jnp.float32)

    @pl.when(step == 0)
    def _():
        first = (lax.axis_index("wide") == 0).astype(jnp.float32)
        total[...] = product + first * bias_ref[...]

    @pl.when(step > 0)
    def _():
        total[...] += product

    @pl.when(step == steps - 1)
    def _():
        blocks, rows = ids_ref.shape[:2]
        low = lax.axis_index("narrow") * total.shape[1]

        def block(w, carry):
            start = pl.multiple_of(w * (rows * fold), rows)
            out_ref[w] = pick_active(total, ids_ref[w] - low, start, rows, fold, top)
            return carry

        lax.fori_loop(0, blocks, block, 0)


def main_kernel(
    W, N, fold, top, chunk,
    part_ref, ids_ref, packed_ids_ref, bias_ref, act_hbm, dec_hbm,
    lat_ref, err_hbm, grad_ref,
    act, dec, slot, wide_in, values, rec, rec_in, err_out, err, lg, lg_packed, grad_in,
    load_sem, out_sem, ws1, wr1, ws2, wr2, ws3, wr3, ns1, nr1, ns2, nr2,
):
    wide, narrow = lax.axis_index("wide"), lax.axis_index("narrow")
    tokens, latents = lat_ref.shape
    own, rows = tokens // N, part_ref.shape[1]
    chunks = err.shape[1] // chunk
    load_act = pltpu.make_async_copy(
        act_hbm.at[pl.ds(pl.multiple_of(narrow * own, own), own)], act, load_sem.at[0]
    )
    load_dec = pltpu.make_async_copy(dec_hbm, dec, load_sem.at[1])
    load_act.start()
    load_dec.start()

    barrier = pltpu.get_barrier_semaphore()
    for d in range(1, W):
        pl.semaphore_signal(barrier, inc=1, device_id={"wide": lax.rem(wide + d, W)}, device_id_type=MESH)
    for d in range(1, N):
        pl.semaphore_signal(barrier, inc=1, device_id={"narrow": lax.rem(narrow + d, N)}, device_id_type=MESH)
    pl.semaphore_wait(barrier, W + N - 2)

    def wide_copy(d, source, target, send, recv):
        return pltpu.make_async_remote_copy(
            src_ref=source, dst_ref=target, send_sem=send.at[d], recv_sem=recv.at[d],
            device_id={"wide": lax.rem(wide + d, W)}, device_id_type=MESH,
        )

    def scatter_copy(d, source, target, send, recv):
        return wide_copy(d, source.at[lax.rem(wide + d, W)], target.at[d], send, recv)

    for d in range(1, W):
        scatter_copy(d, part_ref, wide_in, ws1, wr1).start()

    low = narrow * latents

    def slots_of(i, carry):
        at = pl.ds(pl.multiple_of(i * SUBLANES, SUBLANES), SUBLANES)
        ids = ids_ref[at, :] - low
        place = lax.broadcasted_iota(jnp.int32, (SUBLANES, latents), 1)
        found = jnp.full((SUBLANES, latents), -1, jnp.int32)
        for k in range(top):
            found = jnp.where(ids[:, k : k + 1] == place, k, found)
        slot[at, :] = found
        return carry

    groups = tokens // SUBLANES
    lax.fori_loop(0, groups // 2, slots_of, 0)

    total = part_ref[wide]
    for d in range(1, W):
        scatter_copy(d, part_ref, wide_in, ws1, wr1).wait_recv()
        total = total + wide_in[d]
    values[wide] = total
    for d in range(1, W):
        wide_copy(d, values.at[wide], values.at[wide], ws2, wr2).start()

    lax.fori_loop(groups // 2, groups, slots_of, 0)
    for d in range(1, W):
        wide_copy(d, values.at[wide], values.at[wide], ws2, wr2).wait_recv()

    def spread(table, block, part):
        at = pl.ds(pl.multiple_of((block * fold + part) * rows, rows), rows)
        pieces = []
        for j in range(latents // LANES):
            index = slot[at, j * LANES : (j + 1) * LANES]
            found = lookup(table, jnp.maximum(index, 0) + part * top)
            pieces.append(jnp.where(index >= 0, found, 0.0))
        return jnp.concatenate(pieces, axis=1)

    def fill(block, carry):
        table = values[block]
        both = jnp.concatenate([spread(table, block, part) for part in range(fold)], axis=0)
        at = pl.ds(pl.multiple_of(block * (fold * rows), fold * rows), fold * rows)
        lat_ref[at, :] = both.astype(jnp.bfloat16)
        return carry

    lax.fori_loop(0, W, fill, 0)
    load_act.wait()
    load_dec.wait()

    def narrow_copy(d, source, target, send, recv):
        return pltpu.make_async_remote_copy(
            src_ref=source, dst_ref=target, send_sem=send, recv_sem=recv,
            device_id={"narrow": lax.rem(narrow + d, N)}, device_id_type=MESH,
        )

    def rec_copy(c, d):
        return narrow_copy(d, rec.at[c, lax.rem(narrow + d, N)], rec_in.at[c, d], ns1.at[c, d], nr1.at[c, d])

    def columns(c):
        return pl.ds(pl.multiple_of(c * chunk, chunk), chunk)

    def own_rows(i):
        return pl.ds(pl.multiple_of(i * own, own), own)

    def err_copy(c, d):
        return narrow_copy(d, err_out.at[c, d], err.at[own_rows(narrow), columns(c)], ns2.at[c, d], nr2.at[c, d])

    def decode(c, carry):
        product = jnp.dot(lat_ref[...], dec[:, columns(c)], preferred_element_type=jnp.float32)
        rec[c] = product.astype(jnp.bfloat16).reshape(N, own, chunk)
        for d in range(1, N):
            rec_copy(c, d).start()
        return carry

    lax.fori_loop(0, chunks, decode, 0)

    def combine(c, carry):
        for d in range(1, N):
            rec_copy(c, d).wait_recv()
        shift = bias_ref[:, columns(c)] - act[:, columns(c)].astype(jnp.float32)
        terms = [rec[c, narrow].astype(jnp.float32)]
        terms += [rec_in[c, d].astype(jnp.float32) for d in range(1, N)]
        for e in range(N):
            goal = lax.rem(narrow + e, N)
            back = (N - goal).astype(jnp.float32) * shift
            for d in range(N):
                origin = lax.rem(narrow + N - d, N)
                back = back + (N - jnp.maximum(goal, origin)).astype(jnp.float32) * terms[d]
            back = (back / N).astype(jnp.bfloat16)
            if e == 0:
                err[own_rows(narrow), columns(c)] = back
            else:
                err_out[c, e] = back
                err_copy(c, e).start()
        return carry

    lax.fori_loop(0, chunks, combine, 0)

    def out_copy(c):
        return pltpu.make_async_copy(err.at[:, columns(c)], err_hbm.at[:, columns(c)], out_sem.at[c])

    def contract(c):
        for d in range(1, N):
            err_copy(c, d).wait_recv()
        out_copy(c).start()
        return lax.dot_general(
            err[:, columns(c)], dec[:, columns(c)], (((1,), (1,)), ((), ())), preferred_element_type=jnp.float32
        )

    lg[...] = contract(0)

    def more(c, carry):
        lg[...] += contract(c)
        return carry

    lax.fori_loop(1, chunks, more, 0)

    def pack(w, carry):
        start = pl.multiple_of(w * (rows * fold), rows)
        lg_packed[w] = pick_active(lg, packed_ids_ref[w] - low, start, rows, fold, top)
        return carry

    lax.fori_loop(0, W, pack, 0)
    for d in range(1, W):
        scatter_copy(d, lg_packed, grad_in, ws3, wr3).start()
    total = lg_packed[wide]
    for d in range(1, W):
        scatter_copy(d, lg_packed, grad_in, ws3, wr3).wait_recv()
        total = total + grad_in[d]
    for part in range(fold):
        grad_ref[part * rows : (part + 1) * rows, :] = spread(total, wide, part)

    for d in range(1, W):
        scatter_copy(d, part_ref, wide_in, ws1, wr1).wait_send()
        wide_copy(d, values.at[wide], values.at[wide], ws2, wr2).wait_send()
        scatter_copy(d, lg_packed, grad_in, ws3, wr3).wait_send()

    def drain(c, carry):
        for d in range(1, N):
            rec_copy(c, d).wait_send()
            err_copy(c, d).wait_send()
        out_copy(c).wait()
        return carry

    lax.fori_loop(0, chunks, drain, 0)


def local(activations, enc_weight, enc_bias, dec_weight, dec_bias, active_ids):
    W, N = lax.axis_size("wide"), lax.axis_size("narrow")
    tokens, channels = activations.shape
    latents = enc_weight.shape[1]
    top = active_ids.shape[1]
    fold = max(1, LANES // top)
    rows = tokens // W // fold
    packed_ids = (
        active_ids.reshape(W, fold, rows, top).transpose(0, 2, 1, 3).reshape(W, rows, fold * top)
    )
    depth = min(channels, 512)
    steps = channels // depth
    f32, bf16 = jnp.float32, jnp.bfloat16
    vmem = pl.BlockSpec(memory_space=pltpu.VMEM)
    hbm = pl.BlockSpec(memory_space=pl.ANY)
    flops = 2 * tokens * channels * latents
    packed = pl.pallas_call(
        functools.partial(encode_kernel, steps, fold, top),
        grid=(steps,),
        out_shape=jax.ShapeDtypeStruct((W, rows, fold * top), f32),
        in_specs=[
            pl.BlockSpec((tokens, depth), lambda k: (0, k)),
            pl.BlockSpec((depth, latents), lambda k: (k, 0)),
            pl.BlockSpec((1, latents), lambda k: (0, 0)),
            pl.BlockSpec((W, rows, fold * top), lambda k: (0, 0, 0)),
        ],
        out_specs=pl.BlockSpec((W, rows, fold * top), lambda k: (0, 0, 0)),
        scratch_shapes=[pltpu.VMEM((tokens, latents), f32)],
        cost_estimate=pl.CostEstimate(flops=flops, bytes_accessed=2 * channels * (tokens + latents), transcendentals=0),
        name="encode",
    )(activations, enc_weight, enc_bias.reshape(1, -1), packed_ids)

    chunk = min(channels, 256)
    chunks = channels // chunk
    own = tokens // N
    packed_shape = (W, rows, fold * top)
    dma = pltpu.SemaphoreType.DMA
    lat, err, latent_grad = pl.pallas_call(
        functools.partial(main_kernel, W, N, fold, top, chunk),
        out_shape=(
            jax.ShapeDtypeStruct((tokens, latents), bf16),
            jax.ShapeDtypeStruct((tokens, channels), bf16),
            jax.ShapeDtypeStruct((tokens // W, latents), f32),
        ),
        in_specs=[vmem, vmem, vmem, vmem, hbm, hbm],
        out_specs=(vmem, hbm, vmem),
        scratch_shapes=[
            pltpu.VMEM((own, channels), bf16),
            pltpu.VMEM((latents, channels), bf16),
            pltpu.VMEM((tokens, latents), jnp.int32),
            pltpu.VMEM(packed_shape, f32),
            pltpu.VMEM(packed_shape, f32),
            pltpu.VMEM((chunks, N, own, chunk), bf16),
            pltpu.VMEM((chunks, N, own, chunk), bf16),
            pltpu.VMEM((chunks, N, own, chunk), bf16),
            pltpu.VMEM((tokens, channels), bf16),
            pltpu.VMEM((tokens, latents), f32),
            pltpu.VMEM(packed_shape, f32),
            pltpu.VMEM(packed_shape, f32),
            dma((2,)), dma((chunks,)),
            dma((W,)), dma((W,)), dma((W,)), dma((W,)), dma((W,)), dma((W,)),
            dma((chunks, N)), dma((chunks, N)), dma((chunks, N)), dma((chunks, N)),
        ],
        compiler_params=pltpu.CompilerParams(collective_id=0, has_side_effects=True, vmem_limit_bytes=56 * 2**20),
        cost_estimate=pl.CostEstimate(flops=2 * flops, bytes_accessed=2 * channels * (2 * tokens + latents), transcendentals=0),
        name="exchange",
    )(packed, active_ids, packed_ids, dec_bias.reshape(1, -1), activations, dec_weight)
    dec_grad = lax.dot_general(lat, err, (((0,), (0,)), ((), ())), preferred_element_type=f32).astype(bf16)
    return dec_grad, latent_grad


def solution(mesh):
    in_specs = (
        P(None, "wide"),
        P("wide", "narrow"),
        P("narrow"),
        P("narrow", "wide"),
        P("wide"),
        P(),
    )
    out_specs = (P("narrow", "wide"), P("wide", "narrow"))
    return jax.shard_map(local, mesh=mesh, in_specs=in_specs, out_specs=out_specs, check_vma=False)
```

time: 489 us -> 96.3 us (0.20)
  waiting for transfers between devices: 277 us -> 0 us
  local copies, waits for them, and re-layouts: 125 us -> 2.78 us
  Pallas kernels: 0 us -> 86.3 us
  other arithmetic: 50.6 us -> 0 us
  matrix products: 21.8 us -> 6.35 us
  between operations: 14 us -> 0.67 us
    all_gather x2 -> x0, waiting for transfers between devices: 178 us -> none  [prefix(): lax.all_gather(part.astype(kind), axis)]
    unnamed x20 -> x6, local copies, waits for them, and re-layouts: 124 us -> 1.74 us
    pallas_call x0 -> x2, Pallas kernels: none -> 86.3 us  [the longest x1 78 us: local(): pl.pallas_call(functools.partial(main_kernel, W, N, fold, top, chunk), ou...]
    psum x2 -> x0, waiting for transfers between devices: 67.5 us -> none  [the longest x1 67.5 us: local(): weighted_sum = lax.psum((groups - position) * recon_part, 'narrow')]
    select_n x4 -> x0, other arithmetic: 39.3 us -> none  [hop(): return jax.tree.map(lambda a, b: jnp.where(reached, a, b), new, before)]
    reduce_scatter x1 -> x0, waiting for transfers between devices: 30.2 us -> none  [local(): lax.psum_scatter(lax.dot_general(errors, dec_weight, (((1,), (1,)), ((),...]
    dot_general x4 -> x1, matrix products: 21.8 us -> 6.35 us  [local(): lax.dot_general(lat, err, (((0,), (0,)), ((), ())), preferred_element_typ...]
    convert_element_type x2 -> x0, other arithmetic: 9.41 us -> none  [the longest x1 7.16 us: local(): errors = (suffix / groups).astype(jnp.bfloat16)]
  transfers between devices with their start and end apart: 5 -> 0, of which waited for: 4 -> 0; matrix products, arithmetic and copies ran while one was open for 35% -> 0% of each run, Pallas kernels for 0% -> 0%
where the time goes in v1:
time: 96.3 us; the launch traced here: 96.1 us
  Pallas kernels  86.3 us (90%)
  matrix products  6.35 us (7%)
  local copies, waits for them, and re-layouts  2.78 us (3%)
    pallas_call x1, Pallas kernels, local(): pl.pallas_call(functools.partial(main_kernel, W, N, fold, top, chunk), ou...  78 us
    pallas_call x1, Pallas kernels, local(): pl.pallas_call(functools.partial(encode_kernel, steps, fold, top), grid=(...  8.27 us
    dot_general x1, matrix products, local(): lax.dot_general(lat, err, (((0,), (0,)), ((), ())), preferred_element_typ...  6.35 us

profile of v1, /device:TPU:0, one launch (start us, length us, event | category | flops | bytes accessed | tf_op | source)
XLA Modules:
  0.0 96.1 jit_solution(10513410992310970412)
XLA Ops:
  0.6 1.0 %copy.10.ids_ref = s32[512,64]{1,0:T(8,128)S(1)} copy(s32[512,64]{0,1:T(8,128)} %param.11) | data formatting | bytes 262144 | tf_op args[5]
  1.7 0.0 copy-start
  1.7 0.2 copy.11
  1.9 0.8 reshape.18.ids_ref.packed_ids_ref
  2.7 8.3 %encode.1.part_ref = f32[8,32,128]{2,1,0:T(8,128)} custom-call(bf16[512,2048]{1,0:T(8,128)(2,1)} %act_hbm.1, bf16[2048,1024]{1,0:T(8,128)(2,1)} %enc_ref.1, f32[1,1024]{1,0:T(1,128)} %bitcast.9, s32[8,32,128]{2,1,0:T(8,128)} %reshape.18.ids_ref.packed_ids_ref), custom_call_target="tpu_custom_call" | custom-call | flops 2147483648 | bytes 6291456 | tf_op jit(solution)/shard_map/encode/pallas_call | solution.py:256
  11.0 0.0 copy-done
  11.0 78.0 %exchange.1 = (bf16[512,1024]{1,0:T(8,128)(2,1)}, bf16[512,2048]{1,0:T(8,128)(2,1)}, f32[64,1024]{1,0:T(8,128)}) custom-call(f32[8,32,128]{2,1,0:T(8,128)} %encode.1.part_ref, s32[512,64]{1,0:T(8,128)} %copy-done, s32[8,32,128]{2,1,0:T(8,128)} %reshape.18.ids_ref.packed_ids_ref, f32[1,2048]{1,0:T(1,128)} %bitcast.8, bf16[512,2048]{1,0:T(8,128)(2,1)} %act_hbm.1, ...), custom_call_target="tpu_custom_call" | custom-call | flops 4294967296 | bytes 8388608 | tf_op jit(solution)/shard_map/exchange/pallas_call | solution.py:277
  89.0 0.0 copy-start.1
  89.0 6.4 %convolution_convert_fusion = bf16[1024,2048]{1,0:T(8,128)(2,1)} fusion(bf16[512,1024]{1,0:T(8,128)(2,1)} %get-tuple-element.5, bf16[512,2048]{1,0:T(8,128)(2,1)} %get-tuple-element.6), kind=kOutput, calls=%fused_computation | convolution fusion | flops 2149580800 | bytes 7340032 | tf_op jit(solution)/shard_map/dot_general | solution.py:307
  95.4 0.0 copy-done.1
  95.4 0.7 copy.14
Async XLA Ops:
  1.7 9.3 %copy-start = (s32[512,64]{1,0:T(8,128)}, s32[512,64]{1,0:T(8,128)S(1)}, u32[]{:S(2)}) copy-start(s32[512,64]{1,0:T(8,128)S(1)} %copy.10.ids_ref) | copy-start | bytes 393220
  89.0 6.4 %copy-start.1 = (f32[64,1024]{1,0:T(8,128)S(1)}, f32[64,1024]{1,0:T(8,128)}, u32[]{:S(2)}) copy-start(f32[64,1024]{1,0:T(8,128)} %get-tuple-element.11) | copy-start | bytes 786436

commit v2 on v1

--- a/solution.py
+++ b/solution.py
@@ -16,7 +16,8 @@
     return jnp.take_along_axis(table, index, axis=1, mode="promise_in_bounds")
 
 
-def pick_active(dense_ref, ids, first_row, rows, fold, top):
+def pick_active(dense_ref, ids_ref, low, first_row, rows, fold, top):
+    ids = jnp.concatenate([ids_ref[pl.ds(first_row + part * rows, rows), :] for part in range(fold)], axis=1) - low
     tile, lane = ids >> 7, ids & (LANES - 1)
     half = lax.broadcasted_iota(jnp.int32, ids.shape, 1) // top
     picked = jnp.zeros(ids.shape, jnp.float32)
@@ -44,12 +45,12 @@
 
     @pl.when(step == steps - 1)
     def _():
-        blocks, rows = ids_ref.shape[:2]
+        blocks, rows = out_ref.shape[:2]
         low = lax.axis_index("narrow") * total.shape[1]
 
         def block(w, carry):
             start = pl.multiple_of(w * (rows * fold), rows)
-            out_ref[w] = pick_active(total, ids_ref[w] - low, start, rows, fold, top)
+            out_ref[w] = pick_active(total, ids_ref, low, start, rows, fold, top)
             return carry
 
         lax.fori_loop(0, blocks, block, 0)
@@ -57,7 +58,7 @@
 
 def main_kernel(
     W, N, fold, top, chunk,
-    part_ref, ids_ref, packed_ids_ref, bias_ref, act_hbm, dec_hbm,
+    part_ref, ids_ref, bias_ref, act_hbm, dec_hbm,
     lat_ref, err_hbm, grad_ref,
     act, dec, slot, wide_in, values, rec, rec_in, err_out, err, lg, lg_packed, grad_in,
     load_sem, out_sem, ws1, wr1, ws2, wr2, ws3, wr3, ns1, nr1, ns2, nr2,
@@ -209,7 +210,7 @@
 
     def pack(w, carry):
         start = pl.multiple_of(w * (rows * fold), rows)
-        lg_packed[w] = pick_active(lg, packed_ids_ref[w] - low, start, rows, fold, top)
+        lg_packed[w] = pick_active(lg, ids_ref, low, start, rows, fold, top)
         return carry
 
     lax.fori_loop(0, W, pack, 0)
@@ -244,9 +245,6 @@
     top = active_ids.shape[1]
     fold = max(1, LANES // top)
     rows = tokens // W // fold
-    packed_ids = (
-        active_ids.reshape(W, fold, rows, top).transpose(0, 2, 1, 3).reshape(W, rows, fold * top)
-    )
     depth = min(channels, 512)
     steps = channels // depth
     f32, bf16 = jnp.float32, jnp.bfloat16
@@ -261,13 +259,13 @@
             pl.BlockSpec((tokens, depth), lambda k: (0, k)),
             pl.BlockSpec((depth, latents), lambda k: (k, 0)),
             pl.BlockSpec((1, latents), lambda k: (0, 0)),
-            pl.BlockSpec((W, rows, fold * top), lambda k: (0, 0, 0)),
+            pl.BlockSpec((tokens, top), lambda k: (0, 0)),
         ],
         out_specs=pl.BlockSpec((W, rows, fold * top), lambda k: (0, 0, 0)),
         scratch_shapes=[pltpu.VMEM((tokens, latents), f32)],
         cost_estimate=pl.CostEstimate(flops=flops, bytes_accessed=2 * channels * (tokens + latents), transcendentals=0),
         name="encode",
-    )(activations, enc_weight, enc_bias.reshape(1, -1), packed_ids)
+    )(activations, enc_weight, enc_bias.reshape(1, -1), active_ids)
 
     chunk = min(channels, 256)
     chunks = channels // chunk
@@ -281,7 +279,7 @@
             jax.ShapeDtypeStruct((tokens, channels), bf16),
             jax.ShapeDtypeStruct((tokens // W, latents), f32),
         ),
-        in_specs=[vmem, vmem, vmem, vmem, hbm, hbm],
+        in_specs=[vmem, vmem, vmem, hbm, hbm],
         out_specs=(vmem, hbm, vmem),
         scratch_shapes=[
             pltpu.VMEM((own, channels), bf16),
@@ -303,7 +301,7 @@
         compiler_params=pltpu.CompilerParams(collective_id=0, has_side_effects=True, vmem_limit_bytes=56 * 2**20),
         cost_estimate=pl.CostEstimate(flops=2 * flops, bytes_accessed=2 * channels * (2 * tokens + latents), transcendentals=0),
         name="exchange",
-    )(packed, active_ids, packed_ids, dec_bias.reshape(1, -1), activations, dec_weight)
+    )(packed, active_ids, dec_bias.reshape(1, -1), activations, dec_weight)
     dec_grad = lax.dot_general(lat, err, (((0,), (0,)), ((), ())), preferred_element_type=f32).astype(bf16)
     return dec_grad, latent_grad
 

time: 96.3 us -> 97.1 us (level)
  Pallas kernels: 86.3 us -> 87.4 us
    unnamed x6 -> x4, local copies, waits for them, and re-layouts: 1.74 us -> 2.45 us
where the time goes in v2:
time: 97.1 us; the launch traced here: 96.8 us
  Pallas kernels  87.4 us (90%)
  matrix products  6.35 us (7%)
  local copies, waits for them, and re-layouts  2.45 us (3%)
    pallas_call x1, Pallas kernels, local(): pl.pallas_call(functools.partial(main_kernel, W, N, fold, top, chunk), ou...  78.6 us
    pallas_call x1, Pallas kernels, local(): pl.pallas_call(functools.partial(encode_kernel, steps, fold, top), grid=(...  8.85 us
    dot_general x1, matrix products, local(): lax.dot_general(lat, err, (((0,), (0,)), ((), ())), preferred_element_typ...  6.35 us
    unnamed x4, local copies, waits for them, and re-layouts  2.45 us

profile of v2, /device:TPU:0, one launch (start us, length us, event | category | flops | bytes accessed | tf_op | source)
XLA Modules:
  0.0 96.8 jit_solution(8805632280320564242)
XLA Ops:
  0.6 1.7 %copy.8.ids_ref = s32[512,64]{1,0:T(8,128)} copy(s32[512,64]{0,1:T(8,128)} %param.11) | data formatting | bytes 262144 | tf_op args[5]
  2.4 8.9 %encode.1.part_ref = f32[8,32,128]{2,1,0:T(8,128)} custom-call(bf16[512,2048]{1,0:T(8,128)(2,1)} %act_hbm.1, bf16[2048,1024]{1,0:T(8,128)(2,1)} %enc_ref.1, f32[1,1024]{1,0:T(1,128)} %bitcast.5, s32[512,64]{1,0:T(8,128)} %copy.8.ids_ref), custom_call_target="tpu_custom_call" | custom-call | flops 2147483648 | bytes 6291456 | tf_op jit(solution)/shard_map/encode/pallas_call | solution.py:254
  11.2 78.6 %exchange.1 = (bf16[512,1024]{1,0:T(8,128)(2,1)}, bf16[512,2048]{1,0:T(8,128)(2,1)}, f32[64,1024]{1,0:T(8,128)}) custom-call(f32[8,32,128]{2,1,0:T(8,128)} %encode.1.part_ref, s32[512,64]{1,0:T(8,128)} %copy.8.ids_ref, f32[1,2048]{1,0:T(1,128)} %bitcast.4, bf16[512,2048]{1,0:T(8,128)(2,1)} %act_hbm.1, bf16[1024,2048]{1,0:T(8,128)(2,1)} %dec_hbm.1), custom_call_target="tpu_custom_call" | custom-call | flops 4294967296 | bytes 8388608 | tf_op jit(solution)/shard_map/exchange/pallas_call | solution.py:275
  89.8 0.0 copy-start
  89.8 6.4 %convolution_convert_fusion = bf16[1024,2048]{1,0:T(8,128)(2,1)} fusion(bf16[512,1024]{1,0:T(8,128)(2,1)} %get-tuple-element.5, bf16[512,2048]{1,0:T(8,128)(2,1)} %get-tuple-element.6), kind=kOutput, calls=%fused_computation | convolution fusion | flops 2149580800 | bytes 7340032 | tf_op jit(solution)/shard_map/dot_general | solution.py:305
  96.1 0.0 copy-done
  96.1 0.7 copy.11
Async XLA Ops:
  89.8 6.4 %copy-start = (f32[64,1024]{1,0:T(8,128)S(1)}, f32[64,1024]{1,0:T(8,128)}, u32[]{:S(2)}) copy-start(f32[64,1024]{1,0:T(8,128)} %get-tuple-element.11) | copy-start | bytes 786436
